TPU v7x, 128 devices: a whole 4x4x4 slice. The times are simulated.
128 devices in a mesh: row: 32 (over z, y, core), col: 4 (over x).
Axes of the slice: x: 4, y: 4, z: 4, core: 2. Of those that a mesh axis runs over, the one named last changes fastest.
Arguments:
- matrix: float32 [1, 32, 512, 8, 4, 512], P(None, 'row', None, None, 'col'), may hold values from -30 to 30, as said below
Outputs:
- factored: float32 [1, 32, 512, 8, 4, 512], P(None, 'row', None, None, 'col')
Inputs may be any that keep to these rules, and one draw needn't show every extreme that they name: matrix is symmetric, positive definite and well conditioned.
All inputs are finite; a program needn't handle non-finite values.
Results may differ from a plain program's by a relative error of at most 0.00013.
Values sent between devices are 32-bit elements; how exact they have to be, the bound alone decides.
A program may use at most 192 MiB of HBM per device.

v0:
```python
import jax
import jax.numpy as jnp
from jax import lax
from jax.sharding import PartitionSpec as P

NB = 512
STEPS = 2


def spread(value, axis, source):
    kept = jnp.where(lax.axis_index(axis) == source, value, 0).astype(value.dtype)
    return lax.psum(kept, axis)


def from_root(shard, axis, root):
    return lax.dynamic_index_in_dim(lax.all_gather(shard, axis), root, 0, keepdims=False)


def trailing_product(column_panel, transposed):
    return jnp.einsum(
        "tan,sbn->tasb",
        column_panel,
        transposed,
        precision=lax.Precision.HIGHEST,
        preferred_element_type=jnp.float32,
    )


def shards(matrix):
    local_rows = matrix.shape[0]
    local_cols = matrix.shape[3]
    blocks = matrix.reshape(local_rows, NB, local_cols, NB)
    row_count = lax.axis_size("row")
    column_count = lax.axis_size("col")
    group_size = row_count // column_count
    row_place = lax.axis_index("row")
    column_place = lax.axis_index("col")
    tile_rows = jnp.arange(local_rows, dtype=jnp.int32) * row_count + row_place
    tile_columns = jnp.arange(local_cols, dtype=jnp.int32) * column_count + column_place
    anchor = jnp.int32(0)

    def fetch_columns(column_panel):
        empty = jnp.zeros((local_rows, group_size, NB, NB), jnp.float32)
        slot_index = row_place // column_count
        holder = row_place % column_count == column_place
        contribution = jnp.where(holder, column_panel, 0.0)
        filled = lax.dynamic_update_slice(
            empty, contribution[:, None], (anchor, slot_index, anchor, anchor)
        )
        gathered = lax.psum(filled, "row")
        return gathered.reshape(local_cols, NB, NB)

    def factor_step(blocks, step):
        root_row = step % row_count
        local_row = step // row_count
        root_col = step % column_count
        local_col = step // column_count
        corner = blocks[local_row, :, local_col, :]
        owner = (row_place == root_row) & (column_place == root_col)
        identity = jnp.eye(NB, dtype=jnp.float32)
        chosen = jnp.where(owner, corner, identity)
        factor_local = jnp.linalg.cholesky(chosen)
        diag_block = spread(factor_local, "row", root_row)
        source = blocks[:, :, local_col, :]
        solved = jax.scipy.linalg.solve_triangular(
            diag_block, source.reshape(local_rows * NB, NB).T, lower=True
        ).T
        solved = solved.reshape(local_rows, NB, NB)
        panel_local = jnp.where((tile_rows > step)[:, None, None], solved, 0.0)
        column_panel = from_root(panel_local, "col", root_col)
        transposed = fetch_columns(column_panel)
        return (diag_block, column_panel, transposed)

    factors = factor_step(blocks, 0)
    for step in range(STEPS):
        diag_block, column_panel, transposed = factors
        write_blocks = blocks
        write_local_row = step // row_count
        write_local_col = step // column_count
        column_now = write_blocks[:, :, write_local_col, :]
        owns_col = column_place == step % column_count
        row_after = (tile_rows > step)[:, None, None]
        row_hit = (tile_rows == step)[:, None, None]
        new_column = jnp.where(
            row_after, column_panel, jnp.where(row_hit, diag_block[None], column_now)
        )
        new_column = jnp.where(owns_col, new_column, column_now)
        write_blocks = write_blocks.at[:, :, write_local_col, :].set(new_column)
        row_now = write_blocks[write_local_row]
        owns_row = row_place == step % row_count
        zero_cols = (tile_columns > step)[None, :, None]
        new_row = jnp.where(owns_row & zero_cols, 0.0, row_now)
        blocks = write_blocks.at[write_local_row].set(new_row)
        if step + 1 < STEPS:
            next_col = (step + 1) // column_count
            single = trailing_product(column_panel, transposed[next_col : next_col + 1])
            blocks = blocks.at[:, :, next_col, :].set(
                blocks[:, :, next_col, :] - single[:, :, 0, :]
            )
            factors = factor_step(blocks, step + 1)
            rest = transposed.at[next_col].set(jnp.zeros((NB, NB), jnp.float32))
            blocks = blocks - trailing_product(column_panel, rest)
        else:
            blocks = blocks - trailing_product(column_panel, transposed)
    return blocks.reshape(matrix.shape)


def solution(mesh):
    in_specs = (P(None, "row", None, None, "col", None),)
    out_specs = P(None, "row", None, None, "col", None)
    return jax.shard_map(shards, mesh=mesh, in_specs=in_specs, out_specs=out_specs, check_vma=False)
```

profile of v0, /device:TPU:1, one launch (start us, length us, event | category | flops | bytes accessed | tf_op | source)
XLA Modules:
  0.0 936.6 jit_solution(8377719153286255205)
XLA Ops:
  6.5 20.5 %copy.2 = f32[1,1,512,8,1,512]{2,5,3,4,1,0:T(8,128)} copy(f32[1,1,512,8,1,512]{5,4,3,2,1,0:T(1,128)} %param.16) | data formatting | bytes 16777216 | tf_op args[0]
  27.1 1.3 convert_select_fusion.1
  28.8 1.5 fusion.5
  30.2 11.7 %cholesky.286 = f32[128,128]{1,0:T(8,128)S(1)} custom-call(f32[128,128]{1,0:T(8,128)S(1)} %cholesky.426), custom_call_target="Cholesky" | custom-call | tf_op jit(solution)/shard_map/jit(cholesky)/cholesky | solution.py:62
  42.1 9.8 %custom-call.27 = f32[1,128,128]{1,2,0:T(8,128)S(1)} custom-call(f32[1,128,128]{2,1,0:T(8,128)S(1)} %get-tuple-element.136), custom_call_target="InvertDiagBlocksLowerTriangular" | custom-call | tf_op jit(solution)/shard_map/jit(cholesky)/cholesky | solution.py:62
  52.7 11.7 %cholesky.305 = f32[128,128]{1,0:T(8,128)S(1)} custom-call(f32[128,128]{1,0:T(8,128)S(1)} %cholesky.430), custom_call_target="Cholesky" | custom-call | tf_op jit(solution)/shard_map/jit(cholesky)/cholesky | solution.py:62
  64.6 10.2 %custom-call.28 = f32[1,128,128]{1,2,0:T(8,128)S(1)} custom-call(f32[1,128,128]{2,1,0:T(8,128)S(1)} %get-tuple-element.134), custom_call_target="InvertDiagBlocksLowerTriangular" | custom-call | tf_op jit(solution)/shard_map/jit(cholesky)/cholesky | solution.py:62
  75.9 11.7 %cholesky.326 = f32[128,128]{1,0:T(8,128)S(1)} custom-call(f32[128,128]{1,0:T(8,128)S(1)} %cholesky.435), custom_call_target="Cholesky" | custom-call | tf_op jit(solution)/shard_map/jit(cholesky)/cholesky | solution.py:62
  87.8 9.8 %custom-call.29 = f32[1,128,128]{1,2,0:T(8,128)S(1)} custom-call(f32[1,128,128]{2,1,0:T(8,128)S(1)} %get-tuple-element.132), custom_call_target="InvertDiagBlocksLowerTriangular" | custom-call | tf_op jit(solution)/shard_map/jit(cholesky)/cholesky | solution.py:62
  98.4 11.9 %cholesky.343 = f32[128,128]{1,0:T(8,128)S(1)} custom-call(f32[128,128]{1,0:T(8,128)S(1)} %convolution_subtract_fusion.12), custom_call_target="Cholesky" | custom-call | tf_op jit(solution)/shard_map/jit(cholesky)/cholesky | solution.py:62
  115.0 1.1 fusion.10
  116.2 1.5 slice_bitcast_fusion.20
  117.7 107.4 %all-reduce.6.cloned.1.call-done = f32[512,512]{0,1:T(8,128)} async-done(((f32[512,512]{0,1:T(8,128)}), f32[512,512]{0,1:T(8,128)}) %all-reduce.6.cloned.1.call-update) | async-done | bytes 1048592 | tf_op jit(solution)/shard_map/psum | solution.py:12
  225.1 1.3 fusion.9
  226.5 8.2 while.10
  227.2 1.3 dynamic-slice.63
  229.2 1.3 dynamic-slice.63
  231.3 1.3 dynamic-slice.63
  233.3 1.3 dynamic-slice.63
  235.4 40.1 %custom-call.30 = f32[4,128,128]{1,2,0:T(8,128)S(1)} custom-call(f32[4,128,128]{2,1,0:T(8,128)} %copy-done.4), custom_call_target="InvertDiagBlocksLowerTriangular" | custom-call | tf_op jit(solution)/shard_map/jit(_solve_triangular)/triangular_solve | solution.py:65
  278.9 1.1 fusion
  280.1 47.6 %all-gather.5.cloned.1.call-done = f32[2048,512]{0,1:T(8,128)} async-done(((f32[512,512]{0,1:T(8,128)}), f32[2048,512]{0,1:T(8,128)}) %all-gather.5.cloned.1.call-update) | async-done | bytes 4194320 | tf_op jit(solution)/shard_map/all_gather | solution.py:16
  327.7 1.3 select_bitcast_fusion.1
  329.3 4.3 broadcast.342
  333.6 1.1 constant_dynamic-update-slice_fusion.3
  335.1 2.6 bitcast_dynamic-update-slice_fusion.4
  337.7 8.5 broadcast_select_fusion
  346.1 109.5 %all-reduce.8.cloned.1.call-done = f32[1,8,512,512]{3,2,1,0:T(8,128)} async-done(((f32[1,8,512,512]{3,2,1,0:T(8,128)}), f32[1,8,512,512]{3,2,1,0:T(8,128)}) %all-reduce.8.cloned.1.call-update) | async-done | bytes 8388624 | tf_op jit(solution)/shard_map/psum | solution.py:50
  455.6 3.7 convert_select_fusion
  461.0 11.7 %cholesky.358 = f32[128,128]{1,0:T(8,128)S(1)} custom-call(f32[128,128]{1,0:T(8,128)S(1)} %cholesky.439), custom_call_target="Cholesky" | custom-call | tf_op jit(solution)/shard_map/jit(cholesky)/cholesky | solution.py:62
  472.9 9.8 %custom-call.31 = f32[1,128,128]{1,2,0:T(8,128)S(1)} custom-call(f32[1,128,128]{2,1,0:T(8,128)S(1)} %get-tuple-element.130), custom_call_target="InvertDiagBlocksLowerTriangular" | custom-call | tf_op jit(solution)/shard_map/jit(cholesky)/cholesky | solution.py:62
  482.7 1.2 fusion.37
  484.1 1.3 convolution_subtract_fusion.7
  485.4 12.1 %cholesky.377 = f32[128,128]{1,0:T(8,128)S(1)} custom-call(f32[128,128]{1,0:T(8,128)S(1)} %cholesky.443), custom_call_target="Cholesky" | custom-call | tf_op jit(solution)/shard_map/jit(cholesky)/cholesky | solution.py:62
  497.6 9.8 %custom-call.32 = f32[1,128,128]{1,2,0:T(8,128)S(1)} custom-call(f32[1,128,128]{2,1,0:T(8,128)S(1)} %get-tuple-element.128), custom_call_target="InvertDiagBlocksLowerTriangular" | custom-call | tf_op jit(solution)/shard_map/jit(cholesky)/cholesky | solution.py:62
  507.9 1.5 convolution_subtract_fusion.9
  509.4 11.7 %cholesky.398 = f32[128,128]{1,0:T(8,128)S(1)} custom-call(f32[128,128]{1,0:T(8,128)S(1)} %cholesky.448), custom_call_target="Cholesky" | custom-call | tf_op jit(solution)/shard_map/jit(cholesky)/cholesky | solution.py:62
  521.3 9.8 %custom-call.33 = f32[1,128,128]{1,2,0:T(8,128)S(1)} custom-call(f32[1,128,128]{2,1,0:T(8,128)S(1)} %get-tuple-element.126), custom_call_target="InvertDiagBlocksLowerTriangular" | custom-call | tf_op jit(solution)/shard_map/jit(cholesky)/cholesky | solution.py:62
  531.4 1.5 convolution_subtract_fusion.11
  532.9 11.7 %cholesky.415 = f32[128,128]{1,0:T(8,128)S(1)} custom-call(f32[128,128]{1,0:T(8,128)S(1)} %convolution_subtract_fusion.11), custom_call_target="Cholesky" | custom-call | tf_op jit(solution)/shard_map/jit(cholesky)/cholesky | solution.py:62
  550.1 1.2 select_select_fusion
  551.4 105.4 %all-reduce.10.cloned.1.call-done = f32[512,512]{0,1:T(8,128)} async-done(((f32[512,512]{0,1:T(8,128)}), f32[512,512]{0,1:T(8,128)}) %all-reduce.10.cloned.1.call-update) | async-done | bytes 1048592 | tf_op jit(solution)/shard_map/psum | solution.py:12
  656.7 1.3 fusion.7
  658.1 8.7 while.11
  658.8 1.4 dynamic-slice.65
  660.9 1.4 dynamic-slice.65
  663.1 1.4 dynamic-slice.65
  665.3 1.4 dynamic-slice.65
  666.8 39.3 %custom-call.34 = f32[4,128,128]{1,2,0:T(8,128)S(1)} custom-call(f32[4,128,128]{2,1,0:T(8,128)S(1)} %get-tuple-element.94), custom_call_target="InvertDiagBlocksLowerTriangular" | custom-call | tf_op jit(solution)/shard_map/jit(_solve_triangular)/triangular_solve | solution.py:65
  709.4 1.4 fusion.49
  710.8 1.1 fusion.1
  712.2 47.4 %all-gather.7.cloned.1.call-done = f32[2048,512]{1,0:T(8,128)} async-done(((f32[512,512]{1,0:T(8,128)}), f32[2048,512]{1,0:T(8,128)}) %all-gather.7.cloned.1.call-update) | async-done | bytes 4194320 | tf_op jit(solution)/shard_map/all_gather | solution.py:16
  759.6 1.3 slice.267
  761.3 1.2 select_bitcast_fusion
  762.4 1.6 copy.32
  764.0 4.3 broadcast.351
  768.3 1.1 constant_dynamic-update-slice_fusion.2
  769.4 1.1 broadcast_dynamic-update-slice_fusion
  771.6 16.7 %bitcast_subtract_fusion = f32[1,512,8,512]{1,3,2,0:T(8,128)S(1)} fusion(f32[1,512,8,512]{1,3,2,0:T(8,128)} %bitcast_dynamic-update-slice_fusion.3, f32[8,512,512]{2,1,0:T(8,128)} %broadcast_dynamic-update-slice_fusion, f32[2048,512]{0,1:T(8,128)} %all-gather.5.cloned.1.call-done), kind=kOutput, calls=%fused_computation.4 | convolution fusion | flops 12886999040 | bytes 26214400 | tf_op jit(solution)/shard_map/tan,sbn->tasb/dot_general | solution.py:20
  788.3 3.4 copy.98
  791.7 1.3 bitcast_dynamic-update-slice_fusion.2
  793.0 97.3 %all-reduce.12.cloned.1.call-done = f32[8,512,512]{2,1,0:T(8,128)} async-done(((f32[8,512,512]{2,1,0:T(8,128)}), f32[8,512,512]{2,1,0:T(8,128)}) %all-reduce.12.cloned.1.call-update) | async-done | bytes 8388624 | tf_op jit(solution)/shard_map/psum | solution.py:50
  890.3 18.7 %subtract_bitcast_fusion = f32[1,1,512,8,1,512]{2,5,3,4,1,0:T(8,128)} fusion(f32[512,8,512]{0,2,1:T(8,128)} %bitcast_dynamic-update-slice_fusion.2, pred[8]{0:T(512)(128)(4,1)S(1)} %compare_and_fusion.1, f32[8,512,512]{2,1,0:T(8,128)} %all-reduce.12.cloned.1.call-done, f32[2048,512]{1,0:T(8,128)} %all-gather.7.cloned.1.call-done), kind=kOutput, calls=%fused_computation.5 | convolution fusion | flops 12889096192 | bytes 26214408 | tf_op jit(solution)/shard_map/tan,sbn->tasb/dot_general | solution.py:20
  909.0 20.5 %copy.35 = f32[1,1,512,8,1,512]{5,4,3,2,1,0:T(1,128)} copy(f32[1,1,512,8,1,512]{2,5,3,4,1,0:T(8,128)} %subtract_bitcast_fusion) | data formatting | bytes 16777216 | tf_op jit(solution)/shard_map/reshape | solution.py:105
  (131 shorter events, 27.0 us)
Async XLA Ops:
  6.5 218.6 %all-reduce.6.cloned.1.call-start = ((), (), s32[]{:S(2)}) async-start(), calls=%async_computation | async-start | bytes 2097152 | tf_op jit(solution)/shard_map/psum | solution.py:12
  116.1 211.6 %all-gather.5.cloned.1.call-start = ((), (), s32[]{:S(2)}) async-start(), calls=%async_computation.4 | async-start | bytes 5242880 | tf_op jit(solution)/shard_map/all_gather | solution.py:16
  234.7 0.7 copy-start.4
  280.0 175.6 %all-reduce.8.cloned.1.call-start = ((), (), s32[]{:S(2)}) async-start(), calls=%async_computation.1 | async-start | bytes 16777216 | tf_op jit(solution)/shard_map/psum | solution.py:50
  329.3 5.7 copy-start
  334.8 321.9 %all-reduce.10.cloned.1.call-start = ((), (), s32[]{:S(2)}) async-start(), calls=%async_computation.2 | async-start | bytes 2097152 | tf_op jit(solution)/shard_map/psum | solution.py:12
  460.0 1.1 copy-start.2
  551.3 208.3 %all-gather.7.cloned.1.call-start = ((), (), s32[]{:S(2)}) async-start(), calls=%async_computation.5 | async-start | bytes 5242880 | tf_op jit(solution)/shard_map/all_gather | solution.py:16
  706.1 1.8 copy-start.3
  712.0 178.4 %all-reduce.12.cloned.1.call-start = ((), (), s32[]{:S(2)}) async-start(), calls=%async_computation.3 | async-start | bytes 16777216 | tf_op jit(solution)/shard_map/psum | solution.py:50
  788.3 3.4 copy-start.1
Sparse Core Ops, SparseCore 0:
  116.2 108.8 all-reduce.5
  280.1 47.4 all-gather.4
  334.9 120.6 all-reduce.7
  551.4 105.2 all-reduce.9
  712.1 47.5 all-gather.6
  769.5 120.7 all-reduce.11
where the time goes:
time: 947 us; the launch traced here: 937 us
  waiting for transfers between devices  515 us (54%)
  other arithmetic  263 us (28%)
  local copies, waits for them, and re-layouts  83.2 us (9%)
  matrix products  55 us (6%)
  between operations  19.6 us (2%)
    psum x2, waiting for transfers between devices, spread(): return lax.psum(kept, axis)  213 us
    psum x2, waiting for transfers between devices, fetch_columns(): gathered = lax.psum(filled, 'row')  207 us
    another operation x29, other arithmetic, factor_step(): factor_local = jnp.linalg.cholesky(chosen)  159 us
    all_gather x2, waiting for transfers between devices, from_root(): lax.all_gather(shard, axis)  95 us
    another operation x5, other arithmetic, factor_step(): jax.scipy.linalg.solve_triangular(diag_block, source.reshape(local_rows *...  82.1 us
    dot_general x3, matrix products, trailing_product(): jnp.einsum('tan,sbn->tasb', column_panel, transposed, precision=lax.Preci...  39.1 us
    unnamed x13, local copies, waits for them, and re-layouts  26 us
    reshape x1, local copies, waits for them, and re-layouts, shards(): return blocks.reshape(matrix.shape)  20.5 us
  transfers between devices with their start and end apart: 6, of which 6 were waited for; matrix products, arithmetic and copies ran while one was open for 4% of the time, Pallas kernels for 0%

commit v1 on v0

--- a/solution.py
+++ b/solution.py
@@ -47,7 +47,12 @@
         filled = lax.dynamic_update_slice(
             empty, contribution[:, None], (anchor, slot_index, anchor, anchor)
         )
-        gathered = lax.psum(filled, "row")
+        lanes = lax.axis_size("row")
+        gathered = filled
+        for src_i in [
+            [(num, num ^ h) for num in range(lanes)] for h in (1, 2, 4, 8, 16) if h < lanes
+        ]:
+            gathered = gathered + lax.ppermute(gathered, "row", src_i)
         return gathered.reshape(local_cols, NB, NB)
 
     def factor_step(blocks, step):

time: 947 us -> 2260 us (2.39)
  waiting for transfers between devices: 515 us -> 1740 us
  other arithmetic: 263 us -> 339 us
    ppermute x0 -> x10, waiting for transfers between devices: none -> 1420 us  [fetch_columns(): gathered = gathered + lax.ppermute(gathered, 'row', src_i)]
    psum x2 -> x0, waiting for transfers between devices: 207 us -> none  [fetch_columns(): gathered = lax.psum(filled, 'row')]
    add x0 -> x9, other arithmetic: none -> 78.1 us  [fetch_columns(): gathered = gathered + lax.ppermute(gathered, 'row', src_i)]
  transfers between devices with their start and end apart: 6 -> 14, of which waited for: 6 -> 14; matrix products, arithmetic and copies ran while one was open for 4% -> 2% of each run, Pallas kernels for 0% -> 0%
where the time goes in v1:
time: 2260 us; the launch traced here: 2250 us
  waiting for transfers between devices  1740 us (77%)
  other arithmetic  339 us (15%)
  local copies, waits for them, and re-layouts  81.3 us (4%)
  matrix products  55.5 us (2%)
    ppermute x10, waiting for transfers between devices, fetch_columns(): gathered = gathered + lax.ppermute(gathered, 'row', src_i)  1420 us
    psum x2, waiting for transfers between devices, spread(): return lax.psum(kept, axis)  217 us
    another operation x29, other arithmetic, factor_step(): factor_local = jnp.linalg.cholesky(chosen)  158 us
    all_gather x2, waiting for transfers between devices, from_root(): lax.all_gather(shard, axis)  95.3 us
    another operation x5, other arithmetic, factor_step(): jax.scipy.linalg.solve_triangular(diag_block, source.reshape(local_rows *...  82.1 us
    add x9, other arithmetic, fetch_columns(): gathered = gathered + lax.ppermute(gathered, 'row', src_i)  78.1 us
  transfers between devices with their start and end apart: 14, of which 14 were waited for; matrix products, arithmetic and copies ran while one was open for 2% of the time, Pallas kernels for 0%

profile of v1, /device:TPU:1, one launch (start us, length us, event | category | flops | bytes accessed | tf_op | source)
XLA Modules:
  0.0 2250.0 jit_solution(12512748190144954325)
XLA Ops:
  6.5 20.5 copy.2
  27.1 1.3 convert_select_fusion.1
  28.8 1.5 fusion.12
  30.2 11.7 cholesky.286
  42.1 9.8 custom-call.27
  52.7 11.7 cholesky.305
  64.6 10.0 custom-call.28
  75.6 11.7 cholesky.326
  87.5 9.8 custom-call.29
  98.1 12.1 cholesky.343
  116.1 1.5 slice_bitcast_fusion.20
  117.6 107.4 %all-reduce.4.cloned.1.call-done = f32[512,512]{0,1:T(8,128)} async-done(((f32[512,512]{0,1:T(8,128)}), f32[512,512]{0,1:T(8,128)}) %all-reduce.4.cloned.1.call-update) | async-done | bytes 1048592 | tf_op jit(solution)/shard_map/psum | solution.py:12
  225.1 1.3 fusion.16
  226.4 9.1 while.10
  227.1 1.5 dynamic-slice.65
  229.4 1.5 dynamic-slice.65
  231.7 1.5 dynamic-slice.65
  233.9 1.5 dynamic-slice.65
  236.2 40.1 %custom-call.30 = f32[4,128,128]{1,2,0:T(8,128)S(1)} custom-call(f32[4,128,128]{2,1,0:T(8,128)} %copy-done.7), custom_call_target="InvertDiagBlocksLowerTriangular" | custom-call | tf_op jit(solution)/shard_map/jit(_solve_triangular)/triangular_solve | solution.py:70
  280.8 47.6 %all-gather.5.cloned.1.call-done = f32[2048,512]{0,1:T(8,128)} async-done(((f32[512,512]{0,1:T(8,128)}), f32[2048,512]{0,1:T(8,128)}) %all-gather.5.cloned.1.call-update) | async-done | bytes 4194320 | tf_op jit(solution)/shard_map/all_gather | solution.py:16
  331.7 12.8 collective-permute-done
  344.7 3.2 copy-done.1
  349.2 180.5 %collective-permute-done.1 = f32[1,8,512,512]{2,3,1,0:T(8,128)} collective-permute-done((f32[1,8,512,512]{2,3,1,0:T(8,128)S(1)}, f32[1,8,512,512]{2,3,1,0:T(8,128)}, u32[]{:S(2)}, u32[]{:S(2)}) %collective-permute-start.1) | collective-permute-done | bytes 8388640 | tf_op jit(solution)/shard_map/ppermute | solution.py:55
  529.7 11.1 add.112
  540.8 2.7 collective-permute-start.2
  543.5 179.9 %collective-permute-done.2 = f32[1,8,512,512]{2,3,1,0:T(8,128)} collective-permute-done((f32[1,8,512,512]{2,3,1,0:T(8,128)}, f32[1,8,512,512]{2,3,1,0:T(8,128)}, u32[]{:S(2)}, u32[]{:S(2)}) %collective-permute-start.2) | collective-permute-done | bytes 8388640 | tf_op jit(solution)/shard_map/ppermute | solution.py:55
  723.4 11.1 add.113
  735.7 179.0 %collective-permute-done.3 = f32[1,8,512,512]{2,3,1,0:T(8,128)} collective-permute-done((f32[1,8,512,512]{2,3,1,0:T(8,128)}, f32[1,8,512,512]{2,3,1,0:T(8,128)}, u32[]{:S(2)}, u32[]{:S(2)}) %collective-permute-start.3) | collective-permute-done | bytes 8388640 | tf_op jit(solution)/shard_map/ppermute | solution.py:55
  914.7 11.1 add.114
  925.8 3.0 collective-permute-start.4
  928.8 2.6 bitcast_dynamic-update-slice_fusion.6
  931.4 8.3 broadcast_select_fusion
  939.7 167.1 %collective-permute-done.4 = f32[1,8,512,512]{2,3,1,0:T(8,128)} collective-permute-done((f32[1,8,512,512]{2,3,1,0:T(8,128)}, f32[1,8,512,512]{2,3,1,0:T(8,128)}, u32[]{:S(2)}, u32[]{:S(2)}) %collective-permute-start.4) | collective-permute-done | bytes 8388640 | tf_op jit(solution)/shard_map/ppermute | solution.py:55
  1106.8 11.1 add.115
  1117.9 3.7 convert_select_fusion
  1123.3 11.7 cholesky.358
  1135.1 10.2 custom-call.31
  1148.0 11.7 cholesky.377
  1159.8 9.8 custom-call.32
  1170.1 1.5 convolution_subtract_fusion.9
  1171.6 11.7 cholesky.398
  1183.5 10.0 custom-call.33
  1195.1 11.7 cholesky.415
  1213.1 109.2 %all-reduce.6.cloned.1.call-done = f32[512,512]{0,1:T(8,128)} async-done(((f32[512,512]{0,1:T(8,128)}), f32[512,512]{0,1:T(8,128)}) %all-reduce.6.cloned.1.call-update) | async-done | bytes 1048592 | tf_op jit(solution)/shard_map/psum | solution.py:12
  1322.3 1.3 fusion.14
  1323.7 8.1 while.11
  1331.7 39.3 %custom-call.34 = f32[4,128,128]{1,2,0:T(8,128)S(1)} custom-call(f32[4,128,128]{2,1,0:T(8,128)S(1)} %get-tuple-element.94), custom_call_target="InvertDiagBlocksLowerTriangular" | custom-call | tf_op jit(solution)/shard_map/jit(_solve_triangular)/triangular_solve | solution.py:70
  1374.3 1.4 fusion.56
  1376.9 47.7 %all-gather.7.cloned.1.call-done = f32[2048,512]{1,0:T(8,128)} async-done(((f32[512,512]{1,0:T(8,128)}), f32[2048,512]{1,0:T(8,128)}) %all-gather.7.cloned.1.call-update) | async-done | bytes 4194320 | tf_op jit(solution)/shard_map/all_gather | solution.py:16
  1428.3 12.8 collective-permute-done.5
  1441.4 3.2 copy-done
  1445.8 180.5 %collective-permute-done.6 = f32[1,8,512,512]{2,3,1,0:T(8,128)} collective-permute-done((f32[1,8,512,512]{2,3,1,0:T(8,128)S(1)}, f32[1,8,512,512]{2,3,1,0:T(8,128)}, u32[]{:S(2)}, u32[]{:S(2)}) %collective-permute-start.6) | collective-permute-done | bytes 8388640 | tf_op jit(solution)/shard_map/ppermute | solution.py:55
  1626.4 11.1 add.117
  1637.4 2.9 collective-permute-start.7
  1640.4 179.9 %collective-permute-done.7 = f32[1,8,512,512]{2,3,1,0:T(8,128)} collective-permute-done((f32[1,8,512,512]{2,3,1,0:T(8,128)}, f32[1,8,512,512]{2,3,1,0:T(8,128)}, u32[]{:S(2)}, u32[]{:S(2)}) %collective-permute-start.7) | collective-permute-done | bytes 8388640 | tf_op jit(solution)/shard_map/ppermute | solution.py:55
  1820.2 11.1 add.118
  1832.6 179.0 %collective-permute-done.8 = f32[1,8,512,512]{2,3,1,0:T(8,128)} collective-permute-done((f32[1,8,512,512]{2,3,1,0:T(8,128)}, f32[1,8,512,512]{2,3,1,0:T(8,128)}, u32[]{:S(2)}, u32[]{:S(2)}) %collective-permute-start.8) | collective-permute-done | bytes 8388640 | tf_op jit(solution)/shard_map/ppermute | solution.py:55
  2011.6 11.1 add.119
  2022.6 2.9 collective-permute-start.9
  2027.7 17.1 bitcast_subtract_fusion
  2044.8 4.3 copy.100
  2050.4 153.2 %collective-permute-done.9 = f32[1,8,512,512]{2,3,1,0:T(8,128)} collective-permute-done((f32[1,8,512,512]{2,3,1,0:T(8,128)}, f32[1,8,512,512]{2,3,1,0:T(8,128)}, u32[]{:S(2)}, u32[]{:S(2)}) %collective-permute-start.9) | collective-permute-done | bytes 8388640 | tf_op jit(solution)/shard_map/ppermute | solution.py:55
  2203.5 19.0 subtract_bitcast_fusion
  2222.6 20.5 copy.35
  (161 shorter events, 53.7 us)
Async XLA Ops:
  6.5 218.5 %all-reduce.4.cloned.1.call-start = ((), (), s32[]{:S(2)}) async-start(), calls=%async_computation | async-start | bytes 2097152 | tf_op jit(solution)/shard_map/psum | solution.py:12
  116.1 212.4 %all-gather.5.cloned.1.call-start = ((), (), s32[]{:S(2)}) async-start(), calls=%async_computation.2 | async-start | bytes 5242880 | tf_op jit(solution)/shard_map/all_gather | solution.py:16
  235.5 0.7 copy-start.7
  280.8 1041.6 %all-reduce.6.cloned.1.call-start = ((), (), s32[]{:S(2)}) async-start(), calls=%async_computation.1 | async-start | bytes 2097152 | tf_op jit(solution)/shard_map/psum | solution.py:12
  328.4 2.2 copy-start.2
  330.7 13.7 collective-permute-start
  344.7 3.2 copy-start.1
  347.9 181.7 %collective-permute-start.1 = (f32[1,8,512,512]{2,3,1,0:T(8,128)S(1)}, f32[1,8,512,512]{2,3,1,0:T(8,128)}, u32[]{:S(2)}, u32[]{:S(2)}) collective-permute-start(f32[1,8,512,512]{2,3,1,0:T(8,128)S(1)} %fusion.11), channel_id=1, source_target_pairs={{0,8},{4,12},{8,0},{12,4},{16,24},{20,28},{24,16},{28,20},{32,40},... | collective-permute-start | bytes 25165832 | tf_op jit(solution)/shard_map/ppermute | solution.py:55
  540.8 182.6 %collective-permute-start.2 = (f32[1,8,512,512]{2,3,1,0:T(8,128)}, f32[1,8,512,512]{2,3,1,0:T(8,128)}, u32[]{:S(2)}, u32[]{:S(2)}) collective-permute-start(f32[1,8,512,512]{2,3,1,0:T(8,128)} %add.112), channel_id=1, source_target_pairs={{0,16},{4,20},{8,24},{12,28},{16,0},{20,4},{24,8},{28,12},{32,48},... | collective-permute-start | bytes 25165832 | tf_op jit(solution)/shard_map/ppermute | solution.py:55
  734.4 194.4 %copy-start.3 = (f32[512,512]{0,1:T(8,128)S(1)}, f32[512,512]{0,1:T(8,128)}, u32[]{:S(2)}) copy-start(f32[512,512]{0,1:T(8,128)} %all-reduce.4.cloned.1.call-done) | copy-start | bytes 3145732
  734.4 180.2 %collective-permute-start.3 = (f32[1,8,512,512]{2,3,1,0:T(8,128)}, f32[1,8,512,512]{2,3,1,0:T(8,128)}, u32[]{:S(2)}, u32[]{:S(2)}) collective-permute-start(f32[1,8,512,512]{2,3,1,0:T(8,128)} %add.113), channel_id=1, source_target_pairs={{0,32},{4,36},{8,40},{12,44},{16,48},{20,52},{24,56},{28,60},{32,0... | collective-permute-start | bytes 25165832 | tf_op jit(solution)/shard_map/ppermute | solution.py:55
  925.8 181.0 %collective-permute-start.4 = (f32[1,8,512,512]{2,3,1,0:T(8,128)}, f32[1,8,512,512]{2,3,1,0:T(8,128)}, u32[]{:S(2)}, u32[]{:S(2)}) collective-permute-start(f32[1,8,512,512]{2,3,1,0:T(8,128)} %add.114), channel_id=1, source_target_pairs={{0,64},{4,68},{8,72},{12,76},{16,80},{20,84},{24,88},{28,92},{32,9... | collective-permute-start | bytes 25165832 | tf_op jit(solution)/shard_map/ppermute | solution.py:55
  1122.2 1.1 copy-start.5
  1213.1 211.6 %all-gather.7.cloned.1.call-start = ((), (), s32[]{:S(2)}) async-start(), calls=%async_computation.3 | async-start | bytes 5242880 | tf_op jit(solution)/shard_map/all_gather | solution.py:16
  1371.1 1.8 copy-start.6
  1427.4 13.7 collective-permute-start.5
  1441.4 3.2 copy-start
  1444.6 181.7 %collective-permute-start.6 = (f32[1,8,512,512]{2,3,1,0:T(8,128)S(1)}, f32[1,8,512,512]{2,3,1,0:T(8,128)}, u32[]{:S(2)}, u32[]{:S(2)}) collective-permute-start(f32[1,8,512,512]{2,3,1,0:T(8,128)S(1)} %fusion.8), channel_id=1, source_target_pairs={{0,8},{4,12},{8,0},{12,4},{16,24},{20,28},{24,16},{28,20},{32,40},... | collective-permute-start | bytes 25165832 | tf_op jit(solution)/shard_map/ppermute | solution.py:55
  1637.4 182.8 %collective-permute-start.7 = (f32[1,8,512,512]{2,3,1,0:T(8,128)}, f32[1,8,512,512]{2,3,1,0:T(8,128)}, u32[]{:S(2)}, u32[]{:S(2)}) collective-permute-start(f32[1,8,512,512]{2,3,1,0:T(8,128)} %add.117), channel_id=1, source_target_pairs={{0,16},{4,20},{8,24},{12,28},{16,0},{20,4},{24,8},{28,12},{32,48},... | collective-permute-start | bytes 25165832 | tf_op jit(solution)/shard_map/ppermute | solution.py:55
  1831.3 180.2 %collective-permute-start.8 = (f32[1,8,512,512]{2,3,1,0:T(8,128)}, f32[1,8,512,512]{2,3,1,0:T(8,128)}, u32[]{:S(2)}, u32[]{:S(2)}) collective-permute-start(f32[1,8,512,512]{2,3,1,0:T(8,128)} %add.118), channel_id=1, source_target_pairs={{0,32},{4,36},{8,40},{12,44},{16,48},{20,52},{24,56},{28,60},{32,0... | collective-permute-start | bytes 25165832 | tf_op jit(solution)/shard_map/ppermute | solution.py:55
  2022.6 180.9 %collective-permute-start.9 = (f32[1,8,512,512]{2,3,1,0:T(8,128)}, f32[1,8,512,512]{2,3,1,0:T(8,128)}, u32[]{:S(2)}, u32[]{:S(2)}) collective-permute-start(f32[1,8,512,512]{2,3,1,0:T(8,128)} %add.119), channel_id=1, source_target_pairs={{0,64},{4,68},{8,72},{12,76},{16,80},{20,84},{24,88},{28,92},{32,9... | collective-permute-start | bytes 25165832 | tf_op jit(solution)/shard_map/ppermute | solution.py:55
  2044.7 158.8 %slice-start = ((s8[8388608]{0:T(1024)(128)(4,1)}), s8[4194304]{0:T(1024)(128)(4,1)S(1)}, s32[]{:S(2)}) async-start(s8[8388608]{0:T(1024)(128)(4,1)} %bitcast.167), calls=%async_computation.4 | async-start | bytes 8388608
  2044.8 4.3 copy-start.4
  2044.8 158.8 %slice-start.1 = ((s8[8388608]{0:T(1024)(128)(4,1)}), s8[4194304]{0:T(1024)(128)(4,1)S(1)}, s32[]{:S(2)}) async-start(s8[8388608]{0:T(1024)(128)(4,1)} %bitcast.167), calls=%async_computation.5 | async-start | bytes 8388608
Sparse Core Ops, SparseCore 0:
  116.2 108.8 all-reduce.3
  280.9 47.4 all-gather.4
  1213.2 109.0 all-reduce.5
  1377.1 47.5 all-gather.6
